TPU v7x, 32 devices: a whole 2x2x4 slice. The times are simulated.
32 devices in a mesh: groups: 2 (over y), cells: 8 (over z, x), side: 2 (over core).
Axes of the slice: x: 2, y: 2, z: 4, core: 2. Of those that a mesh axis runs over, the one named last changes fastest.
Arguments:
- datasets: float32 [2, 2000, 8192], P('side', None, ('groups', 'cells')), parts along dimension 2, may hold values from -6 to 6
- sketch: float32 [64, 8192], P(None, ('groups', 'cells')), parts along dimension 1, may hold values from -6 to 6
Outputs:
- factors: float32 [2, 64, 8192], P('side', None, ('groups', 'cells')), parts along dimension 2
There are 2 independent parts, one for each index of `groups`. A program takes and returns all parts, laid end to end along the dimension named above; each array names one. Nothing has to cross between parts.
All inputs are finite; a program needn't handle non-finite values.
Results may differ from a plain program's by a relative error of at most 0.00009.
Values sent between devices are 32-bit elements; how exact they have to be, the bound alone decides.
A program may use at most 64 MiB of HBM per device.

v0:
```python
import jax
import jax.numpy as jnp
from jax import lax
from jax.sharding import PartitionSpec as P


def from_behind(value, axis, steps):
    count = lax.axis_size(axis)
    initial, last = (max(0, -steps), min(count, count - steps))
    return lax.ppermute(value, axis, [(source, source + steps) for source in range(initial, last)])


def per_device(datasets, sketch):
    high = lax.Precision.HIGHEST
    own_data = datasets[0]
    side_index = lax.axis_index("side")
    cell_count = own_data.shape[1] * lax.axis_size("cells")
    scale = jnp.sqrt(jnp.float32(cell_count))
    partial_value = jnp.dot(sketch, own_data.T, precision=high)
    summed = lax.psum(partial_value, "cells")
    arrived = from_behind(summed, "side", -1)
    panel = jnp.where(side_index == 0, arrived, summed)
    range_rows = jnp.dot(panel, own_data, precision=high)
    gram_part = jnp.dot(range_rows, range_rows.T, precision=high)
    raw_part = jnp.dot(range_rows, own_data.T, precision=high)
    gram, raw_cross = lax.psum((gram_part, raw_part), "cells")
    lower = jnp.linalg.cholesky(gram)
    basis = jax.scipy.linalg.solve_triangular(lower, range_rows, lower=True)
    cross = jax.scipy.linalg.solve_triangular(lower, raw_cross, lower=True)
    received = from_behind(cross, "side", 1)
    projected = jnp.dot(received, own_data, precision=high)
    result = jnp.where(side_index == 0, basis * scale, projected / scale)
    return result[None]


def solution(mesh):
    in_specs = (P("side", None, ("groups", "cells")), P(None, ("groups", "cells")))
    out_specs = P("side", None, ("groups", "cells"))
    return jax.shard_map(
        per_device, mesh=mesh, in_specs=in_specs, out_specs=out_specs, check_vma=False
    )
```

profile of v0, /device:TPU:1, one launch (start us, length us, event | category | flops | bytes accessed | tf_op | source)
XLA Modules:
  0.0 225.6 jit_solution(7290744189002880673)
XLA Ops:
  6.5 0.9 copy-done
  7.4 6.7 %fusion.6 = f32[64,2000]{1,0:T(8,128)} fusion(f32[64,512]{1,0:T(8,128)S(1)} %copy-done, f32[1,2000,512]{2,1,0:T(8,128)} %param.2), kind=kOutput, calls=%fused_computation.6 | convolution fusion | flops 786432000 | bytes 4739072 | tf_op jit(solution)/shard_map/dot_general | solution.py:19
  14.1 0.0 all-reduce.3.cloned.1.call-update
  14.2 0.0 all-reduce.5.cloned.1.call-start
  14.2 73.1 %all-reduce.3.cloned.1.call-done = f32[64,2000]{1,0:T(8,128)} async-done(((f32[64,2000]{1,0:T(8,128)}), f32[64,2000]{1,0:T(8,128)}) %all-reduce.3.cloned.1.call-update) | async-done | bytes 512016 | tf_op jit(solution)/shard_map/psum | solution.py:20
  87.3 4.3 %collective-permute-start = (f32[64,2000]{1,0:T(8,128)}, f32[64,2000]{1,0:T(8,128)S(1)}, u32[]{:S(2)}, u32[]{:S(2)}) collective-permute-start(f32[64,2000]{1,0:T(8,128)} %all-reduce.3.cloned.1.call-done), channel_id=1, source_target_pairs={{1,0},{3,2},{5,4},{7,6},{9,8},{11,10},{13,12},{15,14},{17,16},{19,... | collective-permute-start | bytes 1536008 | tf_op jit(solution)/shard_map/ppermute | solution.py:10
  91.7 0.0 copy-start.1
  91.7 1.7 collective-permute-done
  93.3 4.9 %fusion.4 = f32[64,512]{1,0:T(8,128)S(1)} fusion(f32[1,2000,512]{2,1,0:T(8,128)} %param.2, f32[64,2000]{1,0:T(8,128)S(1)} %collective-permute-done, f32[64,2000]{1,0:T(8,128)} %all-reduce.3.cloned.1.call-done, pred[]{:T(512)S(6)} %eq.4), kind=kOutput, calls=%fused_computation.4 | convolution fusion | flops 786560000 | bytes 5251073 | tf_op jit(solution)/shard_map/dot_general | solution.py:23
  98.3 0.3 fusion.24
  98.5 4.6 %fusion.2 = f32[64,2000]{1,0:T(8,128)} fusion(f32[64,512]{1,0:T(8,128)S(1)} %fusion.4, f32[1,2000,512]{2,1,0:T(8,128)S(1)} %copy-done.1), kind=kOutput, calls=%fused_computation.2 | convolution fusion | flops 786432000 | bytes 4739072 | tf_op jit(solution)/shard_map/dot_general | solution.py:25
  103.1 28.1 %psum.22 = f32[64,64]{0,1:T(8,128)S(1)} all-reduce(f32[64,64]{0,1:T(8,128)S(1)} %fusion.24), channel_id=1, replica_groups=mesh['groups'=2,'cells'=8,'side'=2] {'cells'}, use_global_device_ids=true, to_apply=%region_1.2 | all-reduce | flops 4096 | bytes 32768 | tf_op jit(solution)/shard_map/psum | solution.py:26
  131.3 0.1 copy.4
  131.3 0.0 all-reduce.5.cloned.1.call-update
  131.4 5.8 %cholesky.16 = f32[64,64]{1,0:T(8,128)S(1)} custom-call(f32[64,64]{1,0:T(8,128)S(1)} %fusion.23), custom_call_target="Cholesky" | custom-call | tf_op jit(solution)/shard_map/jit(cholesky)/cholesky | solution.py:27
  137.3 0.6 compare_reduce_fusion
  137.9 0.7 fusion.19
  138.6 4.9 %custom-call.10 = f32[1,64,64]{1,2,0:T(8,128)S(1)} custom-call(f32[1,64,64]{2,1,0:T(8,128)S(1)} %fusion.19), custom_call_target="InvertDiagBlocksLowerTriangular" | custom-call | tf_op jit(solution)/shard_map/jit(_solve_triangular)/triangular_solve | solution.py:28
  143.5 63.1 %all-reduce.5.cloned.1.call-done = f32[64,2000]{1,0:T(8,128)} async-done(((f32[64,2000]{1,0:T(8,128)}), f32[64,2000]{1,0:T(8,128)}) %all-reduce.5.cloned.1.call-update) | async-done | bytes 512016 | tf_op jit(solution)/shard_map/psum | solution.py:26
  206.6 1.7 fusion.20
  208.3 1.3 collective-permute-start.1
  209.6 0.3 convolution_multiply_fusion
  209.9 3.4 %collective-permute-done.1 = f32[64,2000]{1,0:T(8,128)S(1)} collective-permute-done((f32[64,2000]{1,0:T(8,128)S(1)}, f32[64,2000]{1,0:T(8,128)S(1)}, u32[]{:S(2)}, u32[]{:S(2)}) %collective-permute-start.1) | collective-permute-done | bytes 512032 | tf_op jit(solution)/shard_map/ppermute | solution.py:10
  213.3 5.4 %fusion.14 = f32[1,64,512]{2,1,0:T(8,128)} fusion(f32[64,512]{1,0:T(8,128)S(1)} %convolution_multiply_fusion, f32[64,2000]{1,0:T(8,128)S(1)} %collective-permute-done.1, f32[1,2000,512]{2,1,0:T(8,128)} %param.2, pred[]{:T(512)S(6)} %eq.4), kind=kOutput, calls=%fused_computation.10 | convolution fusion | flops 786497536 | bytes 4870145 | tf_op jit(solution)/shard_map/dot_general | solution.py:31
  (5 shorter events, 0.0 us)
Async XLA Ops:
  6.5 0.9 copy-start
  6.5 80.8 %all-reduce.3.cloned.1.call-start = ((), (), s32[]{:S(2)}) async-start(), calls=%async_computation | async-start | bytes 1048576 | tf_op jit(solution)/shard_map/psum | solution.py:20
  14.2 192.4 %all-reduce.5.cloned.1.call-start = ((), (), s32[]{:S(2)}) async-start(), calls=%async_computation.1 | async-start | bytes 1048576 | tf_op jit(solution)/shard_map/psum | solution.py:26
  87.3 6.0 %collective-permute-start = (f32[64,2000]{1,0:T(8,128)}, f32[64,2000]{1,0:T(8,128)S(1)}, u32[]{:S(2)}, u32[]{:S(2)}) collective-permute-start(f32[64,2000]{1,0:T(8,128)} %all-reduce.3.cloned.1.call-done), channel_id=1, source_target_pairs={{1,0},{3,2},{5,4},{7,6},{9,8},{11,10},{13,12},{15,14},{17,16},{19,... | collective-permute-start | bytes 1536008 | tf_op jit(solution)/shard_map/ppermute | solution.py:10
  91.7 6.9 %copy-start.1 = (f32[1,2000,512]{2,1,0:T(8,128)S(1)}, f32[1,2000,512]{2,1,0:T(8,128)}, u32[]{:S(2)}) copy-start(f32[1,2000,512]{2,1,0:T(8,128)} %param.2) | copy-start | bytes 12288004
  208.3 5.1 %collective-permute-start.1 = (f32[64,2000]{1,0:T(8,128)S(1)}, f32[64,2000]{1,0:T(8,128)S(1)}, u32[]{:S(2)}, u32[]{:S(2)}) collective-permute-start(f32[64,2000]{1,0:T(8,128)S(1)} %fusion.20), channel_id=1, source_target_pairs={{0,1},{2,3},{4,5},{6,7},{8,9},{10,11},{12,13},{14,15},{16,17},{18,... | collective-permute-start | bytes 1536008 | tf_op jit(solution)/shard_map/ppermute | solution.py:10
Sparse Core Ops, SparseCore 0:
  14.3 73.0 all-reduce.2
  131.5 75.0 all-reduce.4
where the time goes:
time: 226 us
  waiting for transfers between devices  141 us (62%)
  blocking collectives  28.1 us (12%)
  matrix products  23.9 us (11%)
  between operations  13.5 us (6%)
  other arithmetic  12.1 us (5%)
  starting transfers between devices  5.65 us (2%)
    psum x1, waiting for transfers between devices, per_device(): summed = lax.psum(partial_value, 'cells')  73.1 us
    psum x1, waiting for transfers between devices, per_device(): gram, raw_cross = lax.psum((gram_part, raw_part), 'cells')  63.1 us
    psum x1, blocking collectives, per_device(): gram, raw_cross = lax.psum((gram_part, raw_part), 'cells')  28.1 us
    dot_general x1, matrix products, per_device(): partial_value = jnp.dot(sketch, own_data.T, precision=high)  6.69 us
    another operation x3, other arithmetic, per_device(): lower = jnp.linalg.cholesky(gram)  6.52 us
    ppermute x2, starting transfers between devices, from_behind(): lax.ppermute(value, axis, [(source, source + steps) for source in range(i...  5.61 us
    another operation x2, other arithmetic, per_device(): basis = jax.scipy.linalg.solve_triangular(lower, range_rows, lower=True)  5.55 us
    dot_general x1, matrix products, per_device(): projected = jnp.dot(received, own_data, precision=high)  5.42 us
  transfers between devices with their start and end apart: 4, of which 4 were waited for; matrix products, arithmetic and copies ran while one was open for 5% of the time, Pallas kernels for 0%

commit v1 on v0

v1 whole, which is shorter than its diff:
```python
import functools
import math

import jax
import jax.numpy as jnp
from jax import lax
from jax.experimental import pallas as pl
from jax.experimental.pallas import tpu as pltpu
from jax.sharding import PartitionSpec as P

MESH = pl.DeviceIdType.MESH
F32, BF16 = jnp.float32, jnp.bfloat16
HIGHEST = lax.Precision.HIGHEST
NT = (((1,), (1,)), ((), ()))
NN = (((1,), (0,)), ((), ()))


def each(count, body):
    if count <= 8:
        for index in range(count):
            body(index)
    else:
        lax.fori_loop(0, count, lambda index, carry: (body(index), carry)[1], 0)


def halves(value):
    high = value.astype(BF16)
    low = (value - high.astype(F32)).astype(BF16)
    return high, low


def stacked(value):
    return jnp.concatenate(halves(value), axis=0)


def dot3(small, high, low, dims):
    rows = small.shape[0] // 2
    both = lax.dot_general(small, high, dims, preferred_element_type=F32)
    rest = lax.dot_general(small[:rows], low, dims, preferred_element_type=F32)
    return both[:rows] + (both[rows:] + rest)


def inverse_factor(gram):
    k = gram.shape[0]
    row_ids = lax.broadcasted_iota(jnp.int32, gram.shape, 0)
    lanes = lax.broadcasted_iota(jnp.int32, gram.shape, 1)
    start = jnp.where(lanes < k, (lanes == row_ids).astype(F32), gram)
    step = 8
    blocks = [start[i : i + step] for i in range(0, k, step)]
    ids = lax.broadcasted_iota(jnp.int32, (step, 1), 0)
    for j in range(k):
        b, r = divmod(j, step)
        row = blocks[b][r : r + 1]
        scaled = row / row[:, k + j : k + j + 1]
        for i in range(b, k // step):
            column = blocks[i][:, k + j : k + j + 1]
            if i == b:
                column = jnp.where(ids > r, column, 0.0)
            blocks[i] = blocks[i] - column * scaled
    full = jnp.concatenate(blocks, axis=0)
    pivots = jnp.sum(jnp.where(lanes - k == row_ids, full, 0.0), axis=1, keepdims=True)
    return full / jnp.sqrt(pivots)


def kernel(
    n, owners, chunk, data, sketch, out, stage, drawn, high, low, small, parts, inbox, gathered, acc, grams, inverse,
    load_sem, drawn_sem, part_send, part_recv, gather_send, gather_recv, gram_send, gram_recv, inv_send, inv_recv,
):
    me, side = lax.axis_index("cells"), lax.axis_index("side")
    genes, width = data.shape[1:]
    k = sketch.shape[0]
    is_x, is_y = side == 0, side == 1
    barrier = pltpu.get_barrier_semaphore()

    def device(cell, which):
        return {"cells": cell, "side": which}

    def greet(s):
        cell = lax.rem(me + s + 1, n)
        pl.semaphore_signal(barrier, inc=1, device_id=device(cell, 1 - side), device_id_type=MESH)

        @pl.when(cell != me)
        def _():
            pl.semaphore_signal(barrier, inc=1, device_id=device(cell, side), device_id_type=MESH)

    def chunk_at(s):
        return lax.rem(me + 1 + s, owners)

    def start_of(c):
        return pl.multiple_of(jnp.minimum(c * chunk, genes - chunk), 8)

    def load(c):
        return pltpu.make_async_copy(data.at[0, pl.ds(start_of(c), chunk)], stage.at[c], load_sem.at[c])

    draw = pltpu.make_async_copy(sketch, drawn, drawn_sem)
    draw.start()
    each(owners, lambda s: load(chunk_at(s)).start())
    each(n, greet)

    def prepare(c):
        load(c).wait()
        rows = lax.broadcasted_iota(jnp.int32, (chunk, width), 0)
        value = jnp.where(rows >= c * chunk - start_of(c), stage[c], 0.0)
        high[c], low[c] = halves(value)

    def part_copy(c):
        return pltpu.make_async_remote_copy(
            src_ref=parts.at[c], dst_ref=inbox.at[me], send_sem=part_send.at[c], recv_sem=part_recv.at[me],
            device_id=device(c, 1 - side), device_id_type=MESH,
        )

    def part_arrival(i):
        return pltpu.make_async_remote_copy(
            src_ref=parts.at[0], dst_ref=inbox.at[i], send_sem=part_send.at[0], recv_sem=part_recv.at[i],
            device_id=device(i, 1 - side), device_id_type=MESH,
        )

    def gather_copy(cell, slot, which):
        return pltpu.make_async_remote_copy(
            src_ref=gathered.at[slot], dst_ref=gathered.at[slot], send_sem=gather_send.at[which],
            recv_sem=gather_recv.at[slot], device_id=device(cell, side), device_id_type=MESH,
        )

    def gram_copy(cell, slot, which):
        return pltpu.make_async_remote_copy(
            src_ref=grams.at[slot], dst_ref=grams.at[slot], send_sem=gram_send.at[which],
            recv_sem=gram_recv.at[slot], device_id=device(cell, side), device_id_type=MESH,
        )

    inverse_copy = pltpu.make_async_remote_copy(
        src_ref=inverse, dst_ref=inverse, send_sem=inv_send, recv_sem=inv_recv,
        device_id=device(me, 1 - side), device_id_type=MESH,
    )

    def scatter(s):
        c = chunk_at(s)
        parts[c] = dot3(small[...], high[c], low[c], NT)
        part_copy(c).start()

    draw.wait()

    @pl.when(is_x)
    def _():
        each(owners, lambda s: prepare(chunk_at(s)))

    @pl.when(is_y)
    def _():
        small[...] = stacked(drawn[...])
        prepare(chunk_at(0))

    pl.semaphore_wait(barrier, 2 * n - 1)

    @pl.when(is_y)
    def _():
        scatter(0)

        def onward(s):
            prepare(chunk_at(s + 1))
            scatter(s + 1)

        each(owners - 1, onward)

    @pl.when(me < owners)
    def _():
        first = lax.rem(me - 1 + n, n)
        part_arrival(first).wait_recv()
        gathered[me] = inbox[first]

        def add(s):
            i = lax.rem(me - 2 - s + 2 * n, n)
            part_arrival(i).wait_recv()
            gathered[me] += inbox[i]

        each(n - 1, add)
        each(n - 1, lambda s: gather_copy(lax.rem(me + 1 + s, n), me, s).start())

    acc[...] = jnp.zeros_like(acc)

    def collect(s):
        c = lax.rem(lax.rem(me, owners) - s + owners, owners)

        @pl.when(c != me)
        def _():
            gather_copy(me, c, 0).wait_recv()

        acc[...] += dot3(stacked(gathered[c]), high[c], low[c], NN)

    each(owners, collect)

    @pl.when(is_x)
    def _():
        range_rows = acc[...]
        small[...] = stacked(range_rows)
        grams[me] = lax.dot_general(
            range_rows, jnp.concatenate([range_rows, range_rows], axis=0), NT,
            precision=HIGHEST, preferred_element_type=F32,
        )
        each(n - 1, lambda s: gram_copy(lax.rem(me + 1 + s, n), me, s).start())
        each(owners, scatter)

        def arrive(s):
            gram_copy(me, lax.rem(me - 1 - s + n, n), 0).wait_recv()

        each(n - 1, arrive)
        inverse[...] = grams[0]

        def add(i):
            inverse[...] += grams[i + 1]

        each(n - 1, add)
        inverse[...] = inverse_factor(inverse[...])
        inverse_copy.start()

    @pl.when(is_y)
    def _():
        inverse_copy.wait_recv()

    scale = math.sqrt(width * n)
    factor = jnp.where(is_x, scale, 1.0 / scale).astype(F32)
    out[0] = factor * lax.dot_general(
        inverse[:, :k], acc[...], NN, precision=HIGHEST, preferred_element_type=F32
    )

    each(owners, lambda s: part_copy(chunk_at(s)).wait_send())

    @pl.when(me < owners)
    def _():
        each(n - 1, lambda s: gather_copy(lax.rem(me + 1 + s, n), me, s).wait_send())

    @pl.when(is_x)
    def _():
        each(n - 1, lambda s: gram_copy(lax.rem(me + 1 + s, n), me, s).wait_send())
        inverse_copy.wait_send()


def solution(mesh):
    n = mesh.shape["cells"]

    def per_device(datasets, sketch):
        genes, width = datasets.shape[1:]
        k = sketch.shape[0]
        chunk = 128 * -(-genes // (128 * n))
        owners = -(-genes // chunk)
        dma = pltpu.SemaphoreType.DMA
        return pl.pallas_call(
            functools.partial(kernel, n, owners, chunk),
            out_shape=jax.ShapeDtypeStruct((1, k, width), F32),
            in_specs=[pl.BlockSpec(memory_space=pl.ANY)] * 2,
            out_specs=pl.BlockSpec(memory_space=pltpu.VMEM),
            scratch_shapes=[
                pltpu.VMEM((owners, chunk, width), F32),
                pltpu.VMEM((k, width), F32),
                pltpu.VMEM((owners, chunk, width), BF16),
                pltpu.VMEM((owners, chunk, width), BF16),
                pltpu.VMEM((2 * k, width), BF16),
                pltpu.VMEM((owners, k, chunk), F32),
                pltpu.VMEM((n, k, chunk), F32),
                pltpu.VMEM((owners, k, chunk), F32),
                pltpu.VMEM((k, width), F32),
                pltpu.VMEM((n, k, 2 * k), F32),
                pltpu.VMEM((k, 2 * k), F32),
                dma((owners,)), dma,
                dma((owners,)), dma((n,)),
                dma((n,)), dma((owners,)),
                dma((n,)), dma((n,)),
                dma, dma,
            ],
            compiler_params=pltpu.CompilerParams(collective_id=0, has_side_effects=True),
            name="power_pass",
        )(datasets, sketch)

    spec = P("side", None, ("groups", "cells"))
    return jax.shard_map(
        per_device, mesh=mesh, in_specs=(spec, P(None, ("groups", "cells"))), out_specs=spec, check_vma=False
    )
```

time: 226 us -> 42.7 us (0.19)
  the two profiles are of different devices: /device:TPU:1 before, /device:TPU:29 now
where the time goes in v1:
time: 42.7 us; the launch traced here: 42.5 us
  Pallas kernels  41 us (96%)
  local copies, waits for them, and re-layouts  1.57 us (4%)
    pallas_call x1, Pallas kernels, per_device(): pl.pallas_call(functools.partial(kernel, n, owners, chunk), out_shape=jax...  41 us
    unnamed x1, local copies, waits for them, and re-layouts  1.57 us

profile of v1, /device:TPU:29, one launch (start us, length us, event | category | flops | bytes accessed | tf_op | source)
XLA Modules:
  0.0 42.5 jit_solution(8282638782943956371)
XLA Ops:
  0.0 41.0 %power_pass.1 = f32[1,64,512]{2,1,0:T(8,128)} custom-call(f32[1,2000,512]{2,1,0:T(8,128)} %data.1, f32[64,512]{1,0:T(8,128)} %sketch.1), custom_call_target="tpu_custom_call" | custom-call | tf_op jit(solution)/shard_map/power_pass/pallas_call | solution.py:245
  41.0 1.6 %copy.4 = f32[1,64,512]{2,1,0:T(8,128)} copy(f32[1,64,512]{2,1,0:T(8,128)} %power_pass.1) | data formatting | bytes 262144

commit v2 on v1

--- a/solution.py
+++ b/solution.py
@@ -21,6 +21,15 @@
             body(index)
     else:
         lax.fori_loop(0, count, lambda index, carry: (body(index), carry)[1], 0)
+
+
+def flipped(cell, bits, count):
+    bit = 1
+    while bit < count:
+        own = lax.rem(cell // bit, 2)
+        cell = cell + (bits // bit % 2) * (bit - 2 * bit * own)
+        bit *= 2
+    return cell
 
 
 def halves(value):
@@ -63,8 +72,8 @@
 
 
 def kernel(
-    n, owners, chunk, data, sketch, out, stage, drawn, high, low, small, parts, inbox, gathered, acc, grams, inverse,
-    load_sem, drawn_sem, part_send, part_recv, gather_send, gather_recv, gram_send, gram_recv, inv_send, inv_recv,
+    n, owners, chunk, data, sketch, out, stage, drawn, high, low, small, parts, inbox, gathered, acc, grams, total, inverse,
+    passing, load_sem, drawn_sem, pass_send, pass_recv, part_send, part_recv, gather_send, gather_recv, gram_send, gram_recv, inv_send, inv_recv,
 ):
     me, side = lax.axis_index("cells"), lax.axis_index("side")
     genes, width = data.shape[1:]
@@ -83,8 +92,36 @@
         def _():
             pl.semaphore_signal(barrier, inc=1, device_id=device(cell, side), device_id_type=MESH)
 
+    relayed = owners == n == 8
+    far, far_across = n // 2, n // 2 + 1
+
+    def cell_at(s):
+        return flipped(me, s, n) if relayed else lax.rem(me + s, n)
+
+    relay_sums, relay_gathers = relayed, relayed
+    part_order = sum_order = gather_order = collect_order = None
+    if relayed:
+        part_order = ((5, 6, 7, 2, 3, 1, 0, 4), (5, 2, 3, 6, 7, 1, 0, 4)) if relay_sums else (2, 3, 4, 5, 6, 7, 1, 0)
+        sum_order = (0, 1, 2, 3, 6, 7, 4) if relay_sums else (0, 1, 2, 3, 4, 5, 6, 7)
+        gather_order = ((4, 6, 7, 2, 3, 1), (4, 2, 3, 6, 7, 1)) if relay_gathers else (2, 3, 4, 5, 6, 7, 1)
+        collect_order = (0, 1, 4, 2, 3, 6, 7, 5) if relay_gathers else (0, 1, 2, 3, 4, 5, 6, 7)
+
+    def through(order, count, body, start=0):
+        if order is None:
+            each(count - start, lambda s: body(s + start))
+        elif isinstance(order[0], tuple):
+            inner = (me >= 2) & (me < 6)
+            for test, own_order in zip((inner, jnp.logical_not(inner)), order):
+
+                @pl.when(test)
+                def _():
+                    through(own_order, count, body, start)
+        else:
+            for s in order:
+                body(s)
+
     def chunk_at(s):
-        return lax.rem(me + 1 + s, owners)
+        return cell_at(s) if relayed else lax.rem(me + 1 + s, owners)
 
     def start_of(c):
         return pl.multiple_of(jnp.minimum(c * chunk, genes - chunk), 8)
@@ -94,7 +131,7 @@
 
     draw = pltpu.make_async_copy(sketch, drawn, drawn_sem)
     draw.start()
-    each(owners, lambda s: load(chunk_at(s)).start())
+    through(part_order, owners, lambda s: load(chunk_at(s)).start())
     each(n, greet)
 
     def prepare(c):
@@ -132,83 +169,109 @@
         device_id=device(me, 1 - side), device_id_type=MESH,
     )
 
-    def scatter(s):
+    def work_out(s):
         c = chunk_at(s)
         parts[c] = dot3(small[...], high[c], low[c], NT)
-        part_copy(c).start()
+
+    relay_part = pltpu.make_async_remote_copy(
+        src_ref=parts.at[cell_at(far_across)], dst_ref=passing, send_sem=pass_send, recv_sem=pass_recv,
+        device_id=device(cell_at(1), side), device_id_type=MESH,
+    )
+
+    def send(s):
+        if relay_sums and s == far_across:
+            relay_part.start()
+            return
+        if relay_sums and s == far:
+            relay_part.wait_recv()
+            parts[chunk_at(s)] += passing[...]
+        part_copy(chunk_at(s)).start()
+
+    def scatter(s):
+        work_out(s)
+        send(s)
+
+    def prepare_and_work_out(s):
+        prepare(chunk_at(s))
+        work_out(s)
 
     draw.wait()
 
     @pl.when(is_x)
     def _():
-        each(owners, lambda s: prepare(chunk_at(s)))
+        through(part_order, owners, lambda s: prepare(chunk_at(s)))
 
     @pl.when(is_y)
     def _():
         small[...] = stacked(drawn[...])
-        prepare(chunk_at(0))
+        through(part_order, owners, prepare_and_work_out)
 
     pl.semaphore_wait(barrier, 2 * n - 1)
 
     @pl.when(is_y)
     def _():
-        scatter(0)
-
-        def onward(s):
-            prepare(chunk_at(s + 1))
-            scatter(s + 1)
-
-        each(owners - 1, onward)
+        through(part_order, owners, send)
 
     @pl.when(me < owners)
     def _():
-        first = lax.rem(me - 1 + n, n)
-        part_arrival(first).wait_recv()
-        gathered[me] = inbox[first]
-
         def add(s):
-            i = lax.rem(me - 2 - s + 2 * n, n)
+            i = cell_at(s)
             part_arrival(i).wait_recv()
-            gathered[me] += inbox[i]
-
-        each(n - 1, add)
-        each(n - 1, lambda s: gather_copy(lax.rem(me + 1 + s, n), me, s).start())
+            if isinstance(s, int) and s == 0:
+                gathered[me] = inbox[i]
+            else:
+                gathered[me] += inbox[i]
+
+        if relayed:
+            through(sum_order, n, add)
+        else:
+            add(0)
+            each(n - 1, lambda s: add(s + 1))
+        through(gather_order, n, lambda s: gather_copy(cell_at(s), me, s).start(), 1)
 
     acc[...] = jnp.zeros_like(acc)
 
+    relay_gather = gather_copy(cell_at(1), cell_at(far), 0) if relay_gathers else None
+
     def collect(s):
-        c = lax.rem(lax.rem(me, owners) - s + owners, owners)
+        c = cell_at(s) if relayed else lax.rem(lax.rem(me, owners) - s + owners, owners)
 
         @pl.when(c != me)
         def _():
             gather_copy(me, c, 0).wait_recv()
 
+        if relay_gathers and s == far:
+            relay_gather.start()
         acc[...] += dot3(stacked(gathered[c]), high[c], low[c], NN)
 
-    each(owners, collect)
+    through(collect_order, owners, collect)
 
     @pl.when(is_x)
     def _():
         range_rows = acc[...]
         small[...] = stacked(range_rows)
-        grams[me] = lax.dot_general(
+        twice = lax.dot_general(
             range_rows, jnp.concatenate([range_rows, range_rows], axis=0), NT,
             precision=HIGHEST, preferred_element_type=F32,
         )
+        left = lax.broadcasted_iota(jnp.int32, grams.shape[1:], 1) < k
+        grams[me] = jnp.where(left, twice[: k // 2], twice[k // 2 :])
         each(n - 1, lambda s: gram_copy(lax.rem(me + 1 + s, n), me, s).start())
-        each(owners, scatter)
+        through(part_order, owners, scatter)
 
         def arrive(s):
             gram_copy(me, lax.rem(me - 1 - s + n, n), 0).wait_recv()
 
         each(n - 1, arrive)
-        inverse[...] = grams[0]
+        total[...] = grams[0]
 
         def add(i):
-            inverse[...] += grams[i + 1]
+            total[...] += grams[i + 1]
 
         each(n - 1, add)
-        inverse[...] = inverse_factor(inverse[...])
+        bottom = total[...]
+        gram = jnp.concatenate([pltpu.roll(bottom, k, axis=1), bottom], axis=0)
+        inverse[...] = inverse_factor(gram)
         inverse_copy.start()
 
     @pl.when(is_y)
@@ -221,11 +284,14 @@
         inverse[:, :k], acc[...], NN, precision=HIGHEST, preferred_element_type=F32
     )
 
-    each(owners, lambda s: part_copy(chunk_at(s)).wait_send())
+    through(part_order, owners, lambda s: (relay_part if relay_sums and s == far_across else part_copy(chunk_at(s))).wait_send())
 
     @pl.when(me < owners)
     def _():
-        each(n - 1, lambda s: gather_copy(lax.rem(me + 1 + s, n), me, s).wait_send())
+        through(gather_order, n, lambda s: gather_copy(cell_at(s), me, s).wait_send(), 1)
+
+    if relay_gathers:
+        relay_gather.wait_send()
 
     @pl.when(is_x)
     def _():
@@ -257,9 +323,11 @@
                 pltpu.VMEM((n, k, chunk), F32),
                 pltpu.VMEM((owners, k, chunk), F32),
                 pltpu.VMEM((k, width), F32),
-                pltpu.VMEM((n, k, 2 * k), F32),
+                pltpu.VMEM((n, k // 2, 2 * k), F32),
+                pltpu.VMEM((k // 2, 2 * k), F32),
                 pltpu.VMEM((k, 2 * k), F32),
-                dma((owners,)), dma,
+                pltpu.VMEM((k, chunk), F32),
+                dma((owners,)), dma, dma, dma,
                 dma((owners,)), dma((n,)),
                 dma((n,)), dma((owners,)),
                 dma((n,)), dma((n,)),

time: 42.7 us -> 40.1 us (0.939)
  the two profiles are of different devices: /device:TPU:29 before, /device:TPU:1 now
where the time goes in v2:
time: 40.1 us; the launch traced here: 39.9 us
  Pallas kernels  38.3 us (96%)
  local copies, waits for them, and re-layouts  1.57 us (4%)
    pallas_call x1, Pallas kernels, per_device(): pl.pallas_call(functools.partial(kernel, n, owners, chunk), out_shape=jax...  38.3 us
    unnamed x1, local copies, waits for them, and re-layouts  1.57 us

profile of v2, /device:TPU:1, one launch (start us, length us, event | category | flops | bytes accessed | tf_op | source)
XLA Modules:
  0.0 39.9 jit_solution(7643318169321786033)
XLA Ops:
  0.0 38.3 %power_pass.1 = f32[1,64,512]{2,1,0:T(8,128)} custom-call(f32[1,2000,512]{2,1,0:T(8,128)} %data.1, f32[64,512]{1,0:T(8,128)} %sketch.1), custom_call_target="tpu_custom_call" | custom-call | tf_op jit(solution)/shard_map/power_pass/pallas_call | solution.py:311
  38.3 1.6 %copy.4 = f32[1,64,512]{2,1,0:T(8,128)} copy(f32[1,64,512]{2,1,0:T(8,128)} %power_pass.1) | data formatting | bytes 262144

commit v3 on v2

--- a/solution.py
+++ b/solution.py
@@ -280,9 +280,7 @@
 
     scale = math.sqrt(width * n)
     factor = jnp.where(is_x, scale, 1.0 / scale).astype(F32)
-    out[0] = factor * lax.dot_general(
-        inverse[:, :k], acc[...], NN, precision=HIGHEST, preferred_element_type=F32
-    )
+    out[0] = factor * dot3(stacked(inverse[:, :k]), *halves(acc[...]), NN)
 
     through(part_order, owners, lambda s: (relay_part if relay_sums and s == far_across else part_copy(chunk_at(s))).wait_send())
 

time: 40.1 us -> 40 us (level)
  no operation moved by 1% of the time
where the time goes in v3:
time: 40 us; the launch traced here: 39.8 us
  Pallas kernels  38.3 us (96%)
  local copies, waits for them, and re-layouts  1.57 us (4%)
    pallas_call x1, Pallas kernels, per_device(): pl.pallas_call(functools.partial(kernel, n, owners, chunk), out_shape=jax...  38.3 us
    unnamed x1, local copies, waits for them, and re-layouts  1.57 us

profile of v3, /device:TPU:1, one launch (start us, length us, event | category | flops | bytes accessed | tf_op | source)
XLA Modules:
  0.0 39.8 jit_solution(8029252812388510280)
XLA Ops:
  0.0 38.3 %power_pass.1 = f32[1,64,512]{2,1,0:T(8,128)} custom-call(f32[1,2000,512]{2,1,0:T(8,128)} %data.1, f32[64,512]{1,0:T(8,128)} %sketch.1), custom_call_target="tpu_custom_call" | custom-call | tf_op jit(solution)/shard_map/power_pass/pallas_call | solution.py:309
  38.3 1.6 %copy.4 = f32[1,64,512]{2,1,0:T(8,128)} copy(f32[1,64,512]{2,1,0:T(8,128)} %power_pass.1) | data formatting | bytes 262144
